TPU v7x, 256 devices: a whole 4x4x8 slice. The times are simulated.
256 devices in a mesh: days: 128 (over x, z, y), cols: 2 (over core).
Axes of the slice: x: 4, y: 4, z: 8, core: 2. Of those that a mesh axis runs over, the one named last changes fastest.
Arguments:
- cube: float32 [4096, 65536], P('days', 'cols'), may hold values from -800 to 800
- year_id: int32 [4096], P('days'), may hold values from 0 to 2, as said below
- parent: int32 [65536], P('cols'), may hold values from 0 to 511
Outputs:
- running: float32 [4096, 65536], P('days', 'cols')
- rollup: float32 [4096, 512], P('days', 'cols')
Inputs may be any that keep to these rules, and one draw needn't show every extreme that they name: year_id never falls from one day to the next; every year of 0 to 2 has 1 to 3072 days.
All inputs are finite; a program needn't handle non-finite values.
Results may differ from a plain program's by a relative error of at most 0.00012.
Values sent between devices are 32-bit elements; how exact they have to be, the bound alone decides.
A program may use at most 128 MiB of HBM per device.

v0:
```python
import math
import jax
import jax.numpy as jnp
from jax import lax
from jax.sharding import Mesh
from jax.sharding import PartitionSpec as P

PARENTS = 512
DAYS = ("days_0", "days_1", "days_2")


def side_by_side(arrays, axis, dim, along):
    widths = [math.prod(a.shape[along:]) for a in arrays]
    both = jnp.concatenate(
        [a.reshape(*a.shape[:along], w) for a, w in zip(arrays, widths)], axis=along
    )
    out = lax.all_gather(both, axis, axis=dim, tiled=True)
    tiles = jnp.split(out, [sum(widths[:k]) for k in range(1, len(widths))], axis=along)
    return tuple((b.reshape(*out.shape[:along], *a.shape[along:]) for a, b in zip(arrays, tiles)))


def from_everyone(array, axis):
    peers = lax.axis_size(axis)
    return lax.all_to_all(
        jnp.broadcast_to(array[None], (peers, *array.shape)), axis, 0, 0, tiled=True
    )


def over_copies(array, axis):
    everything = from_everyone(array, axis)
    return jnp.sum(everything, axis=0)


def one_axis_at_a_time(array, axes):
    for axis in axes:
        array = lax.psum(array, axis)
    return array


def parent_totals(ytd, parent):
    width = ytd.shape[1]
    block = min(width, 4096)
    nblocks = width // block
    targets = jnp.arange(PARENTS, dtype=jnp.int32)

    def add_block(index, total):
        begin = (index * block).astype(jnp.int32)
        rows = lax.dynamic_slice_in_dim(ytd, begin, block, 1)
        owners = lax.dynamic_slice_in_dim(parent, begin, block, 0)
        onehot = (owners[:, None] == targets[None, :]).astype(jnp.float32)
        return total + jnp.dot(
            rows, onehot, preferred_element_type=jnp.float32, precision=lax.Precision.HIGHEST
        )

    start = jnp.zeros((ytd.shape[0], PARENTS), jnp.float32)
    return lax.fori_loop(0, nblocks, add_block, start)


def body(cube, year_id, parent):
    day_count = cube.shape[0]
    years = year_id.astype(jnp.float32)
    order = jnp.arange(day_count, dtype=jnp.int32)
    lower = jnp.logical_and(order[None, :] <= order[:, None], years[None, :] == years[:, None])
    local = jnp.dot(
        lower.astype(jnp.float32),
        cube,
        preferred_element_type=jnp.float32,
        precision=lax.Precision.HIGHEST,
    )
    first = years[:1]
    last = years[-1:]
    tail = local[-1]
    mine = lax.axis_index(DAYS)
    lasts, tails = side_by_side((last, tail[None, :]), DAYS, 0, 1)
    index = jnp.arange(lasts.shape[0], dtype=jnp.int32)
    weights = jnp.logical_and(index < mine, lasts == first[0]).astype(jnp.float32)
    carried = jnp.dot(
        weights[None, :], tails, preferred_element_type=jnp.float32, precision=lax.Precision.HIGHEST
    )[0]
    ytd = local + jnp.where(years[:, None] == first[0], carried[None, :], 0.0)
    partial_region = parent_totals(ytd, parent)
    total_days = day_count * lax.axis_size(DAYS)
    whole = over_copies(partial_region, "cols")
    squares = one_axis_at_a_time(jnp.sum(whole * whole), DAYS)
    share = PARENTS // lax.axis_size("cols")
    region = lax.dynamic_slice_in_dim(whole, lax.axis_index("cols") * share, share, 1)
    scale = jnp.sqrt(squares / (total_days * PARENTS) + 1e-06)
    return (ytd / scale, region / scale)


def solution(mesh):
    finer = Mesh(
        mesh.devices.reshape(4, 8, 4, mesh.shape["cols"]), ("days_0", "days_1", "days_2", "cols")
    )
    return jax.shard_map(
        body,
        mesh=finer,
        in_specs=(P(DAYS, "cols"), P(DAYS), P("cols")),
        out_specs=(P(DAYS, "cols"), P(DAYS, "cols")),
        check_vma=False,
    )
```

profile of v0, /device:TPU:2, one launch (start us, length us, event | category | flops | bytes accessed | tf_op | source)
XLA Modules:
  0.0 313.8 jit_solution(10033284970401329339)
XLA Ops:
  7.2 0.0 all-gather.3.cloned.1.call-start
  7.2 0.7 convert_element_type.8
  7.9 0.6 fusion.22
  8.5 0.0 copy-start.2
  8.5 4.5 %fusion.10 = f32[32,32768]{1,0:T(8,128)S(1)} fusion(f32[32,32768]{1,0:T(8,128)} %param.5, f32[32]{0:T(128)S(1)} %convert_element_type.8), kind=kOutput, calls=%fused_computation.16 | convolution fusion | flops 402656256 | bytes 8388736 | tf_op jit(solution)/shard_map/dot_general | solution.py:64
  12.9 0.0 copy-start
  12.9 2.0 copy-done
  14.9 0.1 slice.12
  15.1 1.6 maximum_bitcast_fusion
  16.7 0.0 all-gather.3.cloned.1.call-update
  16.8 0.0 copy-done.2
  16.8 0.6 broadcast_compare_fusion
  17.4 152.5 %all-gather.3.cloned.1.call-done = f32[128,1,32769]{2,1,0:T(1,128)} async-done(((f32[1,1,32769]{2,1,0:T(1,128)}), f32[128,1,32769]{2,1,0:T(1,128)}) %all-gather.3.cloned.1.call-update) | async-done | bytes 16777744 | tf_op jit(solution)/shard_map/all_gather | solution.py:17
  169.9 34.6 %copy.7 = f32[128,1,32769]{0,2,1:T(8,128)} copy(f32[128,1,32769]{2,1,0:T(1,128)} %all-gather.3.cloned.1.call-done) | data formatting | bytes 33555456 | tf_op jit(solution)/shard_map/all_gather | solution.py:17
  204.5 0.0 copy-start.1
  204.5 14.8 %fusion.7 = f32[1,32768]{1,0:T(1,128)S(1)} fusion(f32[128,32769]{0,1:T(8,128)} %bitcast.15, f32[]{:T(128)} %bitcast, s32[]{:T(128)S(6)} %add.53), kind=kOutput, calls=%fused_computation.7 | convolution fusion | flops 50332032 | bytes 16909316 | tf_op jit(solution)/shard_map/dot_general | solution.py:77
  219.3 0.0 copy-done.1
  219.3 2.4 select_add_fusion
  221.7 38.6 %while.14 = (s32[]{:T(128)}, f32[32,512]{1,0:T(8,128)S(1)}, f32[32,32768]{1,0:T(8,128)}, s32[32768]{0:T(1024)}, s32[]{:T(128)}, /*index=5*/s32[]{:T(128)}, s32[]{:T(128)}, s32[]{:T(128)}) while((s32[]{:T(128)}, f32[32,512]{1,0:T(8,128)S(1)}, f32[32,32768]{1,0:T(8,128)}, s32[32768]{0:T(1024)}, s32[]{:T(128)}, /*index=5*/s32[]{:T(128)}, ...), condition=%wide.region_1.2_spmd.clone, body=%wide.region_0.1_spmd.clone.sunk | while | flops 807436288 | bytes 704661 | solution.py:56
  221.7 0.7 dynamic_slice.26
  222.4 4.1 %fusion.27 = f32[32,512]{1,0:T(8,128)S(1)} fusion(s32[4096]{0:T(1024)S(1)} %dynamic_slice.26, f32[32,32768]{1,0:T(8,128)} %get-tuple-element.167, s32[]{:T(128)S(6)} %select_n.22, f32[32,512]{1,0:T(8,128)S(1)} %get-tuple-element.158, pred[]{:T(512)S(6)} %compare.3), kind=kOutput, calls=%fused_computation.4.clone.1 | convolution fusion | flops 807436288 | bytes 671749 | tf_op jit(solution)/shard_map/while/body/eval_jaxpr/dot_general | solution.py:51
  226.5 0.7 dynamic_slice.26
  227.3 4.1 %fusion.27 = f32[32,512]{1,0:T(8,128)S(1)} fusion(s32[4096]{0:T(1024)S(1)} %dynamic_slice.26, f32[32,32768]{1,0:T(8,128)} %get-tuple-element.167, s32[]{:T(128)S(6)} %select_n.22, f32[32,512]{1,0:T(8,128)S(1)} %get-tuple-element.158, pred[]{:T(512)S(6)} %compare.3), kind=kOutput, calls=%fused_computation.4.clone.1 | convolution fusion | flops 807436288 | bytes 671749 | tf_op jit(solution)/shard_map/while/body/eval_jaxpr/dot_general | solution.py:51
  231.4 0.7 dynamic_slice.26
  232.1 4.1 %fusion.27 = f32[32,512]{1,0:T(8,128)S(1)} fusion(s32[4096]{0:T(1024)S(1)} %dynamic_slice.26, f32[32,32768]{1,0:T(8,128)} %get-tuple-element.167, s32[]{:T(128)S(6)} %select_n.22, f32[32,512]{1,0:T(8,128)S(1)} %get-tuple-element.158, pred[]{:T(512)S(6)} %compare.3), kind=kOutput, calls=%fused_computation.4.clone.1 | convolution fusion | flops 807436288 | bytes 671749 | tf_op jit(solution)/shard_map/while/body/eval_jaxpr/dot_general | solution.py:51
  236.2 0.7 dynamic_slice.26
  236.9 4.1 %fusion.27 = f32[32,512]{1,0:T(8,128)S(1)} fusion(s32[4096]{0:T(1024)S(1)} %dynamic_slice.26, f32[32,32768]{1,0:T(8,128)} %get-tuple-element.167, s32[]{:T(128)S(6)} %select_n.22, f32[32,512]{1,0:T(8,128)S(1)} %get-tuple-element.158, pred[]{:T(512)S(6)} %compare.3), kind=kOutput, calls=%fused_computation.4.clone.1 | convolution fusion | flops 807436288 | bytes 671749 | tf_op jit(solution)/shard_map/while/body/eval_jaxpr/dot_general | solution.py:51
  241.0 0.7 dynamic_slice.26
  241.8 4.1 %fusion.27 = f32[32,512]{1,0:T(8,128)S(1)} fusion(s32[4096]{0:T(1024)S(1)} %dynamic_slice.26, f32[32,32768]{1,0:T(8,128)} %get-tuple-element.167, s32[]{:T(128)S(6)} %select_n.22, f32[32,512]{1,0:T(8,128)S(1)} %get-tuple-element.158, pred[]{:T(512)S(6)} %compare.3), kind=kOutput, calls=%fused_computation.4.clone.1 | convolution fusion | flops 807436288 | bytes 671749 | tf_op jit(solution)/shard_map/while/body/eval_jaxpr/dot_general | solution.py:51
  245.9 0.7 dynamic_slice.26
  246.6 4.1 %fusion.27 = f32[32,512]{1,0:T(8,128)S(1)} fusion(s32[4096]{0:T(1024)S(1)} %dynamic_slice.26, f32[32,32768]{1,0:T(8,128)} %get-tuple-element.167, s32[]{:T(128)S(6)} %select_n.22, f32[32,512]{1,0:T(8,128)S(1)} %get-tuple-element.158, pred[]{:T(512)S(6)} %compare.3), kind=kOutput, calls=%fused_computation.4.clone.1 | convolution fusion | flops 807436288 | bytes 671749 | tf_op jit(solution)/shard_map/while/body/eval_jaxpr/dot_general | solution.py:51
  250.7 0.7 dynamic_slice.26
  251.4 4.1 %fusion.27 = f32[32,512]{1,0:T(8,128)S(1)} fusion(s32[4096]{0:T(1024)S(1)} %dynamic_slice.26, f32[32,32768]{1,0:T(8,128)} %get-tuple-element.167, s32[]{:T(128)S(6)} %select_n.22, f32[32,512]{1,0:T(8,128)S(1)} %get-tuple-element.158, pred[]{:T(512)S(6)} %compare.3), kind=kOutput, calls=%fused_computation.4.clone.1 | convolution fusion | flops 807436288 | bytes 671749 | tf_op jit(solution)/shard_map/while/body/eval_jaxpr/dot_general | solution.py:51
  255.5 0.7 dynamic_slice.26
  256.3 4.1 %fusion.27 = f32[32,512]{1,0:T(8,128)S(1)} fusion(s32[4096]{0:T(1024)S(1)} %dynamic_slice.26, f32[32,32768]{1,0:T(8,128)} %get-tuple-element.167, s32[]{:T(128)S(6)} %select_n.22, f32[32,512]{1,0:T(8,128)S(1)} %get-tuple-element.158, pred[]{:T(512)S(6)} %compare.3), kind=kOutput, calls=%fused_computation.4.clone.1 | convolution fusion | flops 807436288 | bytes 671749 | tf_op jit(solution)/shard_map/while/body/eval_jaxpr/dot_general | solution.py:51
  260.4 3.8 %all_to_all.5 = f32[2,32,512]{2,1,0:T(8,128)S(1)} all-to-all(f32[2,32,512]{2,1,0:T(8,128)S(1)} %broadcast_in_dim.45), channel_id=1, replica_groups=mesh['days_0'=4,'days_1'=8,'days_2'=4,'cols'=2] {'cols'}, dimensions={0} | all-to-all | bytes 262144 | tf_op jit(solution)/shard_map/all_to_all | solution.py:24
  264.2 0.6 multiply_reduce_fusion
  264.8 9.2 %psum.21 = f32[]{:T(128)} all-reduce(f32[]{:T(128)} %multiply_reduce_fusion), channel_id=1, replica_groups=mesh['days_0'=4,'days_1'=8,'days_2'=4,'cols'=2] {'days_0'}, use_global_device_ids=true, to_apply=%region_4.5 | all-reduce | flops 1 | bytes 8 | tf_op jit(solution)/shard_map/psum | solution.py:36
  274.0 16.1 %psum.22 = f32[]{:T(128)} all-reduce(f32[]{:T(128)} %psum.21), channel_id=1, replica_groups=mesh['days_0'=4,'days_1'=8,'days_2'=4,'cols'=2] {'days_1'}, use_global_device_ids=true, to_apply=%region_5.6 | all-reduce | flops 1 | bytes 8 | tf_op jit(solution)/shard_map/psum | solution.py:36
  290.2 10.8 %psum.23 = f32[]{:T(128)} all-reduce(f32[]{:T(128)} %psum.22), channel_id=1, replica_groups=mesh['days_0'=4,'days_1'=8,'days_2'=4,'cols'=2] {'days_2'}, use_global_device_ids=true, to_apply=%region_6.7 | all-reduce | flops 1 | bytes 8 | tf_op jit(solution)/shard_map/psum | solution.py:36
  301.6 4.7 %broadcast_divide_fusion = f32[32,32768]{1,0:T(8,128)} fusion(f32[]{:T(128)S(6)} %sqrt.3, f32[32,32768]{1,0:T(8,128)} %copy-done, f32[32768]{0:T(1024)S(1)} %bitcast.17, pred[32]{0:T(512)(128)(4,1)S(1)} %broadcast_compare_fusion), kind=kLoop, calls=%fused_computation.10 | loop fusion | flops 3145728 | bytes 8519716 | tf_op jit(solution)/shard_map/div | solution.py:88
  306.3 0.6 dynamic-slice_divide_fusion
  (3 shorter events, 0.0 us)
Async XLA Ops:
  7.2 162.7 %all-gather.3.cloned.1.call-start = ((), (), s32[]{:S(2)}) async-start(), calls=%async_computation.1 | async-start | bytes 16974336 | tf_op jit(solution)/shard_map/all_gather | solution.py:17
  8.5 8.3 %copy-start.2 = (s32[32]{0:T(128)S(1)}, s32[32]{0:T(128)}, u32[]{:S(2)}) copy-start(s32[32]{0:T(128)} %param.6) | copy-start | bytes 388
  12.9 2.0 copy-start
  204.5 14.8 %copy-start.1 = (f32[32,32768]{1,0:T(8,128)S(1)}, f32[32,32768]{1,0:T(8,128)}, u32[]{:S(2)}) copy-start(f32[32,32768]{1,0:T(8,128)} %copy-done) | copy-start | bytes 12582916
Sparse Core Ops, SparseCore 0:
  16.8 152.9 all-gather.2
where the time goes:
time: 316 us; the launch traced here: 314 us
  waiting for transfers between devices  152 us (48%)
  matrix products  52 us (16%)
  local copies, waits for them, and re-layouts  43.1 us (14%)
  blocking collectives  39.9 us (13%)
  between operations  14.8 us (5%)
  other arithmetic  11.2 us (4%)
    all_gather x1, waiting for transfers between devices, side_by_side(): out = lax.all_gather(both, axis, axis=dim, tiled=True)  152 us
    psum x3, blocking collectives, one_axis_at_a_time(): array = lax.psum(array, axis)  36.1 us
    all_gather x1, local copies, waits for them, and re-layouts, side_by_side(): out = lax.all_gather(both, axis, axis=dim, tiled=True)  34.6 us
    dot_general x8, matrix products, add_block(): jnp.dot(rows, onehot, preferred_element_type=jnp.float32, precision=lax.P...  32.7 us
    dot_general x1, matrix products, body(): jnp.dot(weights[None, :], tails, preferred_element_type=jnp.float32, prec...  14.8 us
  transfers between devices with their start and end apart: 1, of which 1 were waited for; matrix products, arithmetic and copies ran while one was open for 0% of the time, Pallas kernels for 0%

commit v1 on v0

--- a/solution.py
+++ b/solution.py
@@ -33,7 +33,8 @@
 
 def one_axis_at_a_time(array, axes):
     for axis in axes:
-        array = lax.psum(array, axis)
+        blocks = lax.all_gather(array, axis, axis=0, tiled=False)
+        array = blocks.sum(axis=0)
     return array
 
 

time: 316 us -> 320 us (1.013)
  local copies, waits for them, and re-layouts: 43.1 us -> 49 us
    psum x3 -> x0, blocking collectives: 36.1 us -> none  [one_axis_at_a_time(): array = lax.psum(array, axis)]
    unnamed x0 -> x3, blocking collectives: none -> 34.2 us
    unnamed x6 -> x21, local copies, waits for them, and re-layouts: 2.02 us -> 7.84 us
  transfers between devices with their start and end apart: 1 -> 1, of which waited for: 1 -> 1; matrix products, arithmetic and copies ran while one was open for 0% -> 1% of each run, Pallas kernels for 0% -> 0%
where the time goes in v1:
time: 320 us; the launch traced here: 318 us
  waiting for transfers between devices  151 us (47%)
  matrix products  51.9 us (16%)
  local copies, waits for them, and re-layouts  49 us (15%)
  blocking collectives  38 us (12%)
  between operations  14.8 us (5%)
  other arithmetic  13 us (4%)
    all_gather x1, waiting for transfers between devices, side_by_side(): out = lax.all_gather(both, axis, axis=dim, tiled=True)  151 us
    all_gather x1, local copies, waits for them, and re-layouts, side_by_side(): out = lax.all_gather(both, axis, axis=dim, tiled=True)  34.6 us
    unnamed x3, blocking collectives  34.2 us
    dot_general x8, matrix products, add_block(): jnp.dot(rows, onehot, preferred_element_type=jnp.float32, precision=lax.P...  32.6 us
    dot_general x1, matrix products, body(): jnp.dot(weights[None, :], tails, preferred_element_type=jnp.float32, prec...  14.8 us
    unnamed x21, local copies, waits for them, and re-layouts  7.84 us
  transfers between devices with their start and end apart: 1, of which 1 were waited for; matrix products, arithmetic and copies ran while one was open for 1% of the time, Pallas kernels for 0%

profile of v1, /device:TPU:2, one launch (start us, length us, event | category | flops | bytes accessed | tf_op | source)
XLA Modules:
  0.0 317.7 jit_solution(806661797640924401)
XLA Ops:
  7.2 0.0 all-gather.3.cloned.1.call-start
  7.2 0.7 convert_element_type.8
  7.9 0.6 fusion.22
  8.5 0.0 copy-start.5
  8.5 0.0 copy-start.4
  8.5 0.0 copy-start.3
  8.5 0.0 copy-start.2
  8.5 4.5 %fusion.10 = f32[32,32768]{1,0:T(8,128)S(1)} fusion(f32[32,32768]{1,0:T(8,128)} %param.5, f32[32]{0:T(128)S(1)} %convert_element_type.8), kind=kOutput, calls=%fused_computation.16 | convolution fusion | flops 402656256 | bytes 8388736 | tf_op jit(solution)/shard_map/dot_general | solution.py:65
  13.0 0.0 copy-start
  13.0 2.0 copy-done
  15.0 0.1 slice.12
  15.1 1.6 maximum_bitcast_fusion
  16.7 0.0 all-gather.3.cloned.1.call-update
  16.8 0.0 copy-done.5
  16.8 0.6 dynamic-slice
  17.4 0.0 copy-done.4
  17.4 0.5 dynamic-slice.1
  18.0 0.0 copy-done.3
  18.0 0.6 dynamic-slice.2
  18.6 0.0 copy-done.2
  18.6 0.6 broadcast_compare_fusion
  19.1 150.8 %all-gather.3.cloned.1.call-done = f32[128,1,32769]{2,1,0:T(1,128)} async-done(((f32[1,1,32769]{2,1,0:T(1,128)}), f32[128,1,32769]{2,1,0:T(1,128)}) %all-gather.3.cloned.1.call-update) | async-done | bytes 16777744 | tf_op jit(solution)/shard_map/all_gather | solution.py:17
  169.9 34.6 %copy.7 = f32[128,1,32769]{0,2,1:T(8,128)} copy(f32[128,1,32769]{2,1,0:T(1,128)} %all-gather.3.cloned.1.call-done) | data formatting | bytes 33555456 | tf_op jit(solution)/shard_map/all_gather | solution.py:17
  204.6 0.0 copy-start.1
  204.6 14.8 %fusion.7 = f32[1,32768]{1,0:T(1,128)S(1)} fusion(f32[128,32769]{0,1:T(8,128)} %bitcast.21, f32[]{:T(128)} %bitcast, s32[]{:T(128)S(6)} %add.47), kind=kOutput, calls=%fused_computation.7 | convolution fusion | flops 50332032 | bytes 16909316 | tf_op jit(solution)/shard_map/dot_general | solution.py:78
  219.3 0.0 copy-done.1
  219.3 2.4 select_add_fusion
  221.7 38.6 %while.14 = (s32[]{:T(128)}, f32[32,512]{1,0:T(8,128)S(1)}, f32[32,32768]{1,0:T(8,128)}, s32[32768]{0:T(1024)}, s32[]{:T(128)}, /*index=5*/s32[]{:T(128)}, s32[]{:T(128)}, s32[]{:T(128)}) while((s32[]{:T(128)}, f32[32,512]{1,0:T(8,128)S(1)}, f32[32,32768]{1,0:T(8,128)}, s32[32768]{0:T(1024)}, s32[]{:T(128)}, /*index=5*/s32[]{:T(128)}, ...), condition=%wide.region_1.2_spmd.clone, body=%wide.region_0.1_spmd.clone.sunk | while | flops 807436288 | bytes 704661 | solution.py:57
  221.7 0.7 dynamic_slice.26
  222.4 4.1 %fusion.27 = f32[32,512]{1,0:T(8,128)S(1)} fusion(s32[4096]{0:T(1024)S(1)} %dynamic_slice.26, f32[32,32768]{1,0:T(8,128)} %get-tuple-element.167, s32[]{:T(128)S(6)} %select_n.22, f32[32,512]{1,0:T(8,128)S(1)} %get-tuple-element.158, pred[]{:T(512)S(6)} %compare.3), kind=kOutput, calls=%fused_computation.4.clone.1 | convolution fusion | flops 807436288 | bytes 671749 | tf_op jit(solution)/shard_map/while/body/eval_jaxpr/dot_general | solution.py:52
  226.5 0.7 dynamic_slice.26
  227.2 4.1 %fusion.27 = f32[32,512]{1,0:T(8,128)S(1)} fusion(s32[4096]{0:T(1024)S(1)} %dynamic_slice.26, f32[32,32768]{1,0:T(8,128)} %get-tuple-element.167, s32[]{:T(128)S(6)} %select_n.22, f32[32,512]{1,0:T(8,128)S(1)} %get-tuple-element.158, pred[]{:T(512)S(6)} %compare.3), kind=kOutput, calls=%fused_computation.4.clone.1 | convolution fusion | flops 807436288 | bytes 671749 | tf_op jit(solution)/shard_map/while/body/eval_jaxpr/dot_general | solution.py:52
  231.3 0.7 dynamic_slice.26
  232.1 4.1 %fusion.27 = f32[32,512]{1,0:T(8,128)S(1)} fusion(s32[4096]{0:T(1024)S(1)} %dynamic_slice.26, f32[32,32768]{1,0:T(8,128)} %get-tuple-element.167, s32[]{:T(128)S(6)} %select_n.22, f32[32,512]{1,0:T(8,128)S(1)} %get-tuple-element.158, pred[]{:T(512)S(6)} %compare.3), kind=kOutput, calls=%fused_computation.4.clone.1 | convolution fusion | flops 807436288 | bytes 671749 | tf_op jit(solution)/shard_map/while/body/eval_jaxpr/dot_general | solution.py:52
  236.2 0.7 dynamic_slice.26
  236.9 4.1 %fusion.27 = f32[32,512]{1,0:T(8,128)S(1)} fusion(s32[4096]{0:T(1024)S(1)} %dynamic_slice.26, f32[32,32768]{1,0:T(8,128)} %get-tuple-element.167, s32[]{:T(128)S(6)} %select_n.22, f32[32,512]{1,0:T(8,128)S(1)} %get-tuple-element.158, pred[]{:T(512)S(6)} %compare.3), kind=kOutput, calls=%fused_computation.4.clone.1 | convolution fusion | flops 807436288 | bytes 671749 | tf_op jit(solution)/shard_map/while/body/eval_jaxpr/dot_general | solution.py:52
  241.0 0.7 dynamic_slice.26
  241.7 4.1 %fusion.27 = f32[32,512]{1,0:T(8,128)S(1)} fusion(s32[4096]{0:T(1024)S(1)} %dynamic_slice.26, f32[32,32768]{1,0:T(8,128)} %get-tuple-element.167, s32[]{:T(128)S(6)} %select_n.22, f32[32,512]{1,0:T(8,128)S(1)} %get-tuple-element.158, pred[]{:T(512)S(6)} %compare.3), kind=kOutput, calls=%fused_computation.4.clone.1 | convolution fusion | flops 807436288 | bytes 671749 | tf_op jit(solution)/shard_map/while/body/eval_jaxpr/dot_general | solution.py:52
  245.8 0.7 dynamic_slice.26
  246.6 4.1 %fusion.27 = f32[32,512]{1,0:T(8,128)S(1)} fusion(s32[4096]{0:T(1024)S(1)} %dynamic_slice.26, f32[32,32768]{1,0:T(8,128)} %get-tuple-element.167, s32[]{:T(128)S(6)} %select_n.22, f32[32,512]{1,0:T(8,128)S(1)} %get-tuple-element.158, pred[]{:T(512)S(6)} %compare.3), kind=kOutput, calls=%fused_computation.4.clone.1 | convolution fusion | flops 807436288 | bytes 671749 | tf_op jit(solution)/shard_map/while/body/eval_jaxpr/dot_general | solution.py:52
  250.7 0.7 dynamic_slice.26
  251.4 4.1 %fusion.27 = f32[32,512]{1,0:T(8,128)S(1)} fusion(s32[4096]{0:T(1024)S(1)} %dynamic_slice.26, f32[32,32768]{1,0:T(8,128)} %get-tuple-element.167, s32[]{:T(128)S(6)} %select_n.22, f32[32,512]{1,0:T(8,128)S(1)} %get-tuple-element.158, pred[]{:T(512)S(6)} %compare.3), kind=kOutput, calls=%fused_computation.4.clone.1 | convolution fusion | flops 807436288 | bytes 671749 | tf_op jit(solution)/shard_map/while/body/eval_jaxpr/dot_general | solution.py:52
  255.5 0.7 dynamic_slice.26
  256.2 4.1 %fusion.27 = f32[32,512]{1,0:T(8,128)S(1)} fusion(s32[4096]{0:T(1024)S(1)} %dynamic_slice.26, f32[32,32768]{1,0:T(8,128)} %get-tuple-element.167, s32[]{:T(128)S(6)} %select_n.22, f32[32,512]{1,0:T(8,128)S(1)} %get-tuple-element.158, pred[]{:T(512)S(6)} %compare.3), kind=kOutput, calls=%fused_computation.4.clone.1 | convolution fusion | flops 807436288 | bytes 671749 | tf_op jit(solution)/shard_map/while/body/eval_jaxpr/dot_general | solution.py:52
  260.3 3.8 %all_to_all.5 = f32[2,32,512]{2,1,0:T(8,128)S(1)} all-to-all(f32[2,32,512]{2,1,0:T(8,128)S(1)} %broadcast_in_dim.45), channel_id=1, replica_groups=mesh['days_0'=4,'days_1'=8,'days_2'=4,'cols'=2] {'cols'}, dimensions={0} | all-to-all | bytes 262144 | tf_op jit(solution)/shard_map/all_to_all | solution.py:24
  264.2 0.6 multiply_reduce_fusion
  264.8 1.4 dynamic-update-slice
  266.2 8.6 %all-reduce = f32[4]{0:T(128)S(1)} all-reduce(f32[4]{0:T(128)S(1)} %dynamic-update-slice), channel_id=1, replica_groups=mesh['days_0'=4,'days_1'=8,'days_2'=4,'cols'=2] {'days_0'}, use_global_device_ids=true, to_apply=%add | all-reduce | flops 4 | bytes 32
  274.8 0.6 reduce_sum.47
  275.4 1.3 dynamic-update-slice.1
  276.7 15.5 %all-reduce.1 = f32[8]{0:T(128)S(1)} all-reduce(f32[8]{0:T(128)S(1)} %dynamic-update-slice.1), channel_id=1, replica_groups=mesh['days_0'=4,'days_1'=8,'days_2'=4,'cols'=2] {'days_1'}, use_global_device_ids=true, to_apply=%add.1 | all-reduce | flops 8 | bytes 64
  292.2 0.6 reduce_sum.48
  292.8 1.4 dynamic-update-slice.2
  294.1 10.1 %all-reduce.2 = f32[4]{0:T(128)S(1)} all-reduce(f32[4]{0:T(128)S(1)} %dynamic-update-slice.2), channel_id=1, replica_groups=mesh['days_0'=4,'days_1'=8,'days_2'=4,'cols'=2] {'days_2'}, use_global_device_ids=true, to_apply=%add.2 | all-reduce | flops 4 | bytes 32
  304.3 0.6 reduce_sum.49
  305.6 4.7 %broadcast_divide_fusion = f32[32,32768]{1,0:T(8,128)} fusion(f32[]{:T(128)S(6)} %sqrt.3, f32[32,32768]{1,0:T(8,128)} %copy-done, f32[32768]{0:T(1024)S(1)} %bitcast.23, pred[32]{0:T(512)(128)(4,1)S(1)} %broadcast_compare_fusion), kind=kLoop, calls=%fused_computation.10 | loop fusion | flops 3145728 | bytes 8519716 | tf_op jit(solution)/shard_map/div | solution.py:89
  310.2 0.6 dynamic-slice_divide_fusion
  (6 shorter events, 0.0 us)
Async XLA Ops:
  7.2 162.8 %all-gather.3.cloned.1.call-start = ((), (), s32[]{:S(2)}) async-start(), calls=%async_computation.1 | async-start | bytes 16974336 | tf_op jit(solution)/shard_map/all_gather | solution.py:17
  8.5 8.3 %copy-start.5 = (u32[256]{0:T(256)S(1)}, u32[256]{0:T(256)}, u32[]{:S(2)}) copy-start(u32[256]{0:T(256)} %constant.66) | copy-start | bytes 3076
  8.5 9.0 %copy-start.4 = (u32[256]{0:T(256)S(1)}, u32[256]{0:T(256)}, u32[]{:S(2)}) copy-start(u32[256]{0:T(256)} %constant.71) | copy-start | bytes 3076
  8.5 9.5 %copy-start.3 = (u32[256]{0:T(256)S(1)}, u32[256]{0:T(256)}, u32[]{:S(2)}) copy-start(u32[256]{0:T(256)} %constant.76) | copy-start | bytes 3076
  8.5 10.1 %copy-start.2 = (s32[32]{0:T(128)S(1)}, s32[32]{0:T(128)}, u32[]{:S(2)}) copy-start(s32[32]{0:T(128)} %param.6) | copy-start | bytes 388
  13.0 2.0 copy-start
  204.6 14.8 %copy-start.1 = (f32[32,32768]{1,0:T(8,128)S(1)}, f32[32,32768]{1,0:T(8,128)}, u32[]{:S(2)}) copy-start(f32[32,32768]{1,0:T(8,128)} %copy-done) | copy-start | bytes 12582916
Sparse Core Ops, SparseCore 0:
  16.9 152.9 all-gather.2
